TPU v7x, 32 devices: a whole 2x2x4 slice. The times are simulated.
32 devices in a mesh: row: 8 (over z, y), col: 4 (over x, core).
Axes of the slice: x: 2, y: 2, z: 4, core: 2. Of those that a mesh axis runs over, the one named last changes fastest.
Arguments:
- right_side: float32 [3, 64, 512], P(None, 'row', 'col'), may hold values from -6 to 6
- viscosity: float32 [64, 512], P('row', 'col'), may hold values from 0.1 to 3
- free_mask: int32 [3, 64, 512], P(None, 'row', 'col'), may hold values 0 or 1
- coarse_basis: float32 [64, 3, 64, 512], P(None, None, 'row', 'col'), may hold values from -6 to 6
- gram_inverse: float32 [64, 64], P('col'), may hold values from -3 to 6, as said below
Outputs:
- solution: float32 [3, 64, 512], P(None, 'row', 'col')
- residual: float32 [3, 64, 512], P(None, 'row', 'col')
Inputs may be any that keep to these rules, and one draw needn't show every extreme that they name: `free_mask`: 1 marks a free velocity unknown, 0 one whose value is prescribed. `gram_inverse`: symmetric positive definite.
All inputs are finite; a program needn't handle non-finite values. No bound on the sum of `free_mask` on one device may be relied on, other than what follows from the above.
Results may differ from a plain program's by a relative error of at most 0.0003.
Values sent between devices are 32-bit elements; how exact they have to be, the bound alone decides.
A program may use at most 64 MiB of HBM per device.

v0:
```python
import math

import jax
import jax.numpy as jnp
from jax import lax
from jax.sharding import PartitionSpec as P

ITERS = 2


def padded_2(shard, sides, width):
    for axis, dim in sides:
        count, length = (lax.axis_size(axis), shard.shape[dim])
        up = [(i, (i + 1) % count) for i in range(count - 1)]
        down = [(j, i) for i, j in up]
        last = lax.slice_in_dim(shard, length - width, length, axis=dim)
        leading = lax.slice_in_dim(shard, 0, width, axis=dim)
        before = lax.ppermute(last, axis, up)
        after = lax.ppermute(leading, axis, down)
        shard = jnp.concatenate([before, shard, after], axis=dim)
    return shard


def on_device(right_side, viscosity, free_mask, coarse_basis, gram_inverse):
    high = lax.Precision.HIGHEST
    components, patch_rows, patch_cols = right_side.shape
    columns = coarse_basis.shape[0]
    unknowns = (
        components * patch_rows * patch_cols * lax.axis_size("row") * lax.axis_size("col") * columns
    )
    coarse_scale = 1.0 / (32.0 * math.sqrt(float(unknowns)))
    viscosity_pad = padded_2(viscosity, (("row", 0), ("col", 1)), 1)
    face_north = 0.5 * (viscosity + viscosity_pad[2:, 1:-1])
    face_south = 0.5 * (viscosity + viscosity_pad[:-2, 1:-1])
    face_east = 0.5 * (viscosity + viscosity_pad[1:-1, 2:])
    face_west = 0.5 * (viscosity + viscosity_pad[1:-1, :-2])
    diagonal = 1.0 + face_north + face_south + face_east + face_west
    unfixed = free_mask.astype(jnp.float32)
    jacobi = unfixed / diagonal + (1.0 - unfixed)
    basis_rows = coarse_basis.reshape(columns, -1)

    def solve_coarse(coarse_dot):
        coeff_part = jnp.dot(gram_inverse, coarse_dot, precision=high) * coarse_scale
        return lax.all_gather(coeff_part, "col", axis=0, tiled=True)

    def precondition(residual, coarse_dot, weighted_sq):
        coeffs = solve_coarse(coarse_dot)
        smoothed = jacobi * residual + jnp.dot(coeffs, basis_rows, precision=high).reshape(
            residual.shape
        )
        return (smoothed, weighted_sq + jnp.dot(coarse_dot, coeffs, precision=high))

    solution = jnp.zeros_like(right_side)
    residual = right_side
    coarse_dot, weighted_sq = lax.psum(
        (
            jnp.dot(basis_rows, residual.reshape(-1), precision=high),
            jnp.sum(jacobi * residual * residual),
        ),
        ("row", "col"),
    )
    direction, energy = precondition(residual, coarse_dot, weighted_sq)
    for iteration in range(ITERS):
        masked = unfixed * direction
        padded = padded_2(masked, (("row", 1), ("col", 2)), 1)
        stencil = diagonal * masked - (
            face_north * padded[:, 2:, 1:-1]
            + face_south * padded[:, :-2, 1:-1]
            + face_east * padded[:, 1:-1, 2:]
            + face_west * padded[:, 1:-1, :-2]
        )
        applied = unfixed * stencil + (1.0 - unfixed) * direction
        if iteration + 1 < ITERS:
            curve_sum, image_coarse, cross_term, image_sq = lax.psum(
                (
                    jnp.sum(direction * applied),
                    jnp.dot(basis_rows, applied.reshape(-1), precision=high),
                    jnp.sum(jacobi * residual * applied),
                    jnp.sum(jacobi * applied * applied),
                ),
                ("row", "col"),
            )
            step_len = energy / curve_sum
            solution = step_len * direction
            residual = residual - step_len * applied
            coarse_dot = coarse_dot - step_len * image_coarse
            weighted_sq = weighted_sq - 2.0 * step_len * cross_term + step_len * step_len * image_sq
            smoothed, energy_new = precondition(residual, coarse_dot, weighted_sq)
            direction = smoothed + energy_new / energy * direction
            energy = energy_new
        else:
            curve_sum = lax.psum(jnp.sum(direction * applied), ("row", "col"))
            step_len = energy / curve_sum
            solution = solution + step_len * direction
            residual = residual - step_len * applied
    return (solution, residual)


def solution(mesh):
    in_specs = (
        P(None, "row", "col"),
        P("row", "col"),
        P(None, "row", "col"),
        P(None, None, "row", "col"),
        P("col", None),
    )
    out_specs = (P(None, "row", "col"), P(None, "row", "col"))
    return jax.shard_map(
        on_device, mesh=mesh, in_specs=in_specs, out_specs=out_specs, check_vma=False
    )
```

profile of v0, /device:TPU:0, one launch (start us, length us, event | category | flops | bytes accessed | tf_op | source)
XLA Modules:
  0.0 198.3 jit_solution(4688476039508117926)
XLA Ops:
  0.6 0.0 copy-start
  0.6 0.8 fusion.55
  1.4 1.3 collective-permute-start
  2.7 5.5 %collective-permute-start.1 = (f32[1,128]{1,0:T(1,128)S(1)}, f32[1,128]{1,0:T(1,128)S(1)}, u32[]{:S(2)}, u32[]{:S(2)}) collective-permute-start(f32[1,128]{1,0:T(1,128)S(1)} %get-tuple-element.33), channel_id=1, source_target_pairs={{0,4},{4,8},{8,12},{12,16},{16,20},{20,24},{24,28},{1,5},{5,9},{9,... | collective-permute-start | bytes 1544 | tf_op jit(solution)/shard_map/ppermute | solution.py:18
  8.2 1.3 copy.32
  9.5 0.0 copy-start.1
  9.5 0.0 copy-start.2
  9.5 0.1 copy.22
  9.7 1.0 copy-done.1
  10.7 0.0 copy-done.2
  10.7 0.7 convolution_bitcast_fusion.3
  11.4 41.9 %psum.50 = f32[64]{0:T(128)S(1)} all-reduce(f32[64]{0:T(128)S(1)} %convolution_bitcast_fusion.3), channel_id=1, replica_groups=mesh['row'=8,'col'=4] {'row','col'}, use_global_device_ids=true, to_apply=%region_2.0 | all-reduce | flops 64 | bytes 512 | tf_op jit(solution)/shard_map/psum | solution.py:55
  53.3 0.0 copy-done
  53.3 0.1 fusion.1
  53.4 0.0 copy-start.5
  53.4 0.7 copy-done.5
  54.1 0.6 dynamic-slice
  55.3 0.2 dynamic-update-slice
  55.5 5.8 %all-reduce = f32[64]{0:T(128)S(1)} all-reduce(f32[64]{0:T(128)S(1)} %dynamic-update-slice), channel_id=1, replica_groups=mesh['row'=8,'col'=4] {'col'}, use_global_device_ids=true, to_apply=%add | all-reduce | flops 64 | bytes 512
  61.3 0.0 copy-start.4
  61.3 0.6 fusion.4
  61.9 0.0 collective-permute-done
  61.9 0.0 collective-permute-done.1
  61.9 0.1 copy-done.4
  62.0 0.0 copy-start.3
  62.0 0.1 fusion.54
  62.1 1.3 collective-permute-start.2
  63.4 3.0 %collective-permute-start.3 = (f32[10,1]{1,0:T(8,128)S(1)}, f32[10,1]{1,0:T(8,128)S(1)}, u32[]{:S(2)}, u32[]{:S(2)}) collective-permute-start(f32[10,1]{1,0:T(8,128)S(1)} %get-tuple-element.31), channel_id=1, source_target_pairs={{0,1},{1,2},{2,3},{4,5},{5,6},{6,7},{8,9},{9,10},{10,11},{12,13},{... | collective-permute-start | bytes 128 | tf_op jit(solution)/shard_map/ppermute | solution.py:18
  66.4 0.0 collective-permute-done.2
  66.5 0.8 collective-permute-done.3
  67.3 0.1 add_add_fusion
  67.3 0.0 copy-done.3
  67.4 1.3 collective-permute-start.4
  68.7 4.8 %collective-permute-start.5 = (f32[3,1,128]{2,1,0:T(1,128)S(1)}, f32[3,1,128]{2,1,0:T(1,128)S(1)}, u32[]{:S(2)}, u32[]{:S(2)}) collective-permute-start(f32[3,1,128]{2,1,0:T(1,128)S(1)} %get-tuple-element.29), channel_id=1, source_target_pairs={{0,4},{4,8},{8,12},{12,16},{16,20},{20,24},{24,28},{1,5},{5,9},{9,... | collective-permute-start | bytes 4616 | tf_op jit(solution)/shard_map/ppermute | solution.py:18
  73.5 0.0 collective-permute-done.4
  73.5 1.3 collective-permute-done.5
  74.8 0.1 fusion.51
  74.9 2.3 %collective-permute-start.7 = (f32[3,10,1]{2,1,0:T(8,128)S(1)}, f32[3,10,1]{2,1,0:T(8,128)S(1)}, u32[]{:S(2)}, u32[]{:S(2)}) collective-permute-start(f32[3,10,1]{2,1,0:T(8,128)S(1)} %get-tuple-element.26), channel_id=1, source_target_pairs={{0,1},{1,2},{2,3},{4,5},{5,6},{6,7},{8,9},{9,10},{10,11},{12,13},{... | collective-permute-start | bytes 368 | tf_op jit(solution)/shard_map/ppermute | solution.py:18
  77.2 1.3 collective-permute-start.6
  78.5 0.7 multiply_reduce_fusion.5
  79.1 0.0 collective-permute-done.7
  79.1 4.0 %collective-permute-done.6 = f32[3,10,1]{2,1,0:T(8,128)S(1)} collective-permute-done((f32[3,10,1]{2,1,0:T(8,128)S(1)}, f32[3,10,1]{2,1,0:T(8,128)S(1)}, u32[]{:S(2)}, u32[]{:S(2)}) %collective-permute-start.6) | collective-permute-done | bytes 152 | tf_op jit(solution)/shard_map/ppermute | solution.py:19
  83.2 0.7 fusion.8
  83.9 0.7 convolution_bitcast_fusion.1
  84.6 42.6 %all-reduce.2 = (f32[64]{0:T(128)S(1)}, f32[]{:T(128)}, f32[]{:T(128)}, f32[]{:T(128)}, f32[]{:T(128)}) all-reduce(f32[64]{0:T(128)S(1)} %convolution_bitcast_fusion.1, f32[]{:T(128)} %get-tuple-element.4, f32[]{:T(128)} %get-tuple-element.5, f32[]{:T(128)} %get-tuple-element.3, ...), channel_id=1, replica_groups=mesh['row'=8,'col'=4] {'row','col'}, use_global_device_ids=true, to_apply=%region_9.0 | all-reduce | flops 68 | bytes 544 | tf_op jit(solution)/shard_map/psum | solution.py:74
  129.1 0.1 fusion
  129.2 0.2 dynamic-update-slice.1
  129.5 7.6 %all-reduce.1 = f32[64]{0:T(128)S(1)} all-reduce(f32[64]{0:T(128)S(1)} %dynamic-update-slice.1), channel_id=1, replica_groups=mesh['row'=8,'col'=4] {'col'}, use_global_device_ids=true, to_apply=%add.1 | all-reduce | flops 64 | bytes 512
  137.1 0.6 multiply_reduce_fusion.4
  137.7 0.6 fusion.2
  140.8 1.3 collective-permute-start.8
  142.1 4.5 %collective-permute-start.9 = (f32[3,1,128]{2,1,0:T(1,128)S(1)}, f32[3,1,128]{2,1,0:T(1,128)S(1)}, u32[]{:S(2)}, u32[]{:S(2)}) collective-permute-start(f32[3,1,128]{2,1,0:T(1,128)S(1)} %get-tuple-element.27), channel_id=1, source_target_pairs={{0,4},{4,8},{8,12},{12,16},{16,20},{20,24},{24,28},{1,5},{5,9},{9,... | collective-permute-start | bytes 4616 | tf_op jit(solution)/shard_map/ppermute | solution.py:18
  146.7 0.0 collective-permute-done.8
  146.7 1.3 collective-permute-done.9
  148.0 0.1 fusion.50
  148.0 1.3 collective-permute-start.11
  149.3 1.3 collective-permute-start.10
  150.6 0.0 collective-permute-done.11
  150.6 2.6 %collective-permute-done.10 = f32[3,10,1]{2,1,0:T(8,128)S(1)} collective-permute-done((f32[3,10,1]{2,1,0:T(8,128)S(1)}, f32[3,10,1]{2,1,0:T(8,128)S(1)}, u32[]{:S(2)}, u32[]{:S(2)}) %collective-permute-start.10) | collective-permute-done | bytes 152 | tf_op jit(solution)/shard_map/ppermute | solution.py:19
  153.3 0.7 multiply_reduce_fusion
  154.0 43.0 %psum.55 = f32[]{:T(128)} all-reduce(f32[]{:T(128)} %get-tuple-element.11), channel_id=1, replica_groups=mesh['row'=8,'col'=4] {'row','col'}, use_global_device_ids=true, to_apply=%region_11.0 | all-reduce | flops 1 | bytes 8 | tf_op jit(solution)/shard_map/psum | solution.py:92
  197.7 0.6 multiply_subtract_fusion
  (9 shorter events, 0.1 us)
Async XLA Ops:
  0.6 52.6 %copy-start = (f32[16,64]{1,0:T(8,128)S(1)}, f32[16,64]{1,0:T(8,128)}, u32[]{:S(2)}) copy-start(f32[16,64]{1,0:T(8,128)} %param.9) | copy-start | bytes 12292
  1.4 60.5 %collective-permute-start = (f32[1,128]{1,0:T(1,128)S(1)}, f32[1,128]{1,0:T(1,128)S(1)}, u32[]{:S(2)}, u32[]{:S(2)}) collective-permute-start(f32[1,128]{1,0:T(1,128)S(1)} %get-tuple-element.34), channel_id=1, source_target_pairs={{4,0},{8,4},{12,8},{16,12},{20,16},{24,20},{28,24},{5,1},{9,5},{13... | collective-permute-start | bytes 1544 | tf_op jit(solution)/shard_map/ppermute | solution.py:19
  2.7 59.2 %collective-permute-start.1 = (f32[1,128]{1,0:T(1,128)S(1)}, f32[1,128]{1,0:T(1,128)S(1)}, u32[]{:S(2)}, u32[]{:S(2)}) collective-permute-start(f32[1,128]{1,0:T(1,128)S(1)} %get-tuple-element.33), channel_id=1, source_target_pairs={{0,4},{4,8},{8,12},{12,16},{16,20},{20,24},{24,28},{1,5},{5,9},{9,... | collective-permute-start | bytes 1544 | tf_op jit(solution)/shard_map/ppermute | solution.py:18
  9.5 1.1 copy-start.1
  9.5 1.1 copy-start.2
  53.4 0.7 copy-start.5
  61.3 0.7 copy-start.4
  62.0 5.3 %copy-start.3 = (s32[3,8,128]{2,1,0:T(8,128)S(1)}, s32[3,8,128]{2,1,0:T(8,128)}, u32[]{:S(2)}) copy-start(s32[3,8,128]{2,1,0:T(8,128)} %param.7) | copy-start | bytes 36868
  62.1 4.3 %collective-permute-start.2 = (f32[10,1]{1,0:T(8,128)S(1)}, f32[10,1]{1,0:T(8,128)S(1)}, u32[]{:S(2)}, u32[]{:S(2)}) collective-permute-start(f32[10,1]{1,0:T(8,128)S(1)} %get-tuple-element.32), channel_id=1, source_target_pairs={{1,0},{2,1},{3,2},{5,4},{6,5},{7,6},{9,8},{10,9},{11,10},{13,12},{... | collective-permute-start | bytes 128 | tf_op jit(solution)/shard_map/ppermute | solution.py:19
  63.4 3.8 %collective-permute-start.3 = (f32[10,1]{1,0:T(8,128)S(1)}, f32[10,1]{1,0:T(8,128)S(1)}, u32[]{:S(2)}, u32[]{:S(2)}) collective-permute-start(f32[10,1]{1,0:T(8,128)S(1)} %get-tuple-element.31), channel_id=1, source_target_pairs={{0,1},{1,2},{2,3},{4,5},{5,6},{6,7},{8,9},{9,10},{10,11},{12,13},{... | collective-permute-start | bytes 128 | tf_op jit(solution)/shard_map/ppermute | solution.py:18
  67.4 6.1 %collective-permute-start.4 = (f32[3,1,128]{2,1,0:T(1,128)S(1)}, f32[3,1,128]{2,1,0:T(1,128)S(1)}, u32[]{:S(2)}, u32[]{:S(2)}) collective-permute-start(f32[3,1,128]{2,1,0:T(1,128)S(1)} %get-tuple-element.30), channel_id=1, source_target_pairs={{4,0},{8,4},{12,8},{16,12},{20,16},{24,20},{28,24},{5,1},{9,5},{13... | collective-permute-start | bytes 4616 | tf_op jit(solution)/shard_map/ppermute | solution.py:19
  68.7 6.1 %collective-permute-start.5 = (f32[3,1,128]{2,1,0:T(1,128)S(1)}, f32[3,1,128]{2,1,0:T(1,128)S(1)}, u32[]{:S(2)}, u32[]{:S(2)}) collective-permute-start(f32[3,1,128]{2,1,0:T(1,128)S(1)} %get-tuple-element.29), channel_id=1, source_target_pairs={{0,4},{4,8},{8,12},{12,16},{16,20},{20,24},{24,28},{1,5},{5,9},{9,... | collective-permute-start | bytes 4616 | tf_op jit(solution)/shard_map/ppermute | solution.py:18
  74.9 4.3 %collective-permute-start.7 = (f32[3,10,1]{2,1,0:T(8,128)S(1)}, f32[3,10,1]{2,1,0:T(8,128)S(1)}, u32[]{:S(2)}, u32[]{:S(2)}) collective-permute-start(f32[3,10,1]{2,1,0:T(8,128)S(1)} %get-tuple-element.26), channel_id=1, source_target_pairs={{0,1},{1,2},{2,3},{4,5},{5,6},{6,7},{8,9},{9,10},{10,11},{12,13},{... | collective-permute-start | bytes 368 | tf_op jit(solution)/shard_map/ppermute | solution.py:18
  77.2 6.0 %collective-permute-start.6 = (f32[3,10,1]{2,1,0:T(8,128)S(1)}, f32[3,10,1]{2,1,0:T(8,128)S(1)}, u32[]{:S(2)}, u32[]{:S(2)}) collective-permute-start(f32[3,10,1]{2,1,0:T(8,128)S(1)} %get-tuple-element.25), channel_id=1, source_target_pairs={{1,0},{2,1},{3,2},{5,4},{6,5},{7,6},{9,8},{10,9},{11,10},{13,12},{... | collective-permute-start | bytes 368 | tf_op jit(solution)/shard_map/ppermute | solution.py:19
  140.8 5.9 %collective-permute-start.8 = (f32[3,1,128]{2,1,0:T(1,128)S(1)}, f32[3,1,128]{2,1,0:T(1,128)S(1)}, u32[]{:S(2)}, u32[]{:S(2)}) collective-permute-start(f32[3,1,128]{2,1,0:T(1,128)S(1)} %get-tuple-element.28), channel_id=1, source_target_pairs={{4,0},{8,4},{12,8},{16,12},{20,16},{24,20},{28,24},{5,1},{9,5},{13... | collective-permute-start | bytes 4616 | tf_op jit(solution)/shard_map/ppermute | solution.py:19
  142.1 5.8 %collective-permute-start.9 = (f32[3,1,128]{2,1,0:T(1,128)S(1)}, f32[3,1,128]{2,1,0:T(1,128)S(1)}, u32[]{:S(2)}, u32[]{:S(2)}) collective-permute-start(f32[3,1,128]{2,1,0:T(1,128)S(1)} %get-tuple-element.27), channel_id=1, source_target_pairs={{0,4},{4,8},{8,12},{12,16},{16,20},{20,24},{24,28},{1,5},{5,9},{9,... | collective-permute-start | bytes 4616 | tf_op jit(solution)/shard_map/ppermute | solution.py:18
  148.0 2.6 %collective-permute-start.11 = (f32[3,10,1]{2,1,0:T(8,128)S(1)}, f32[3,10,1]{2,1,0:T(8,128)S(1)}, u32[]{:S(2)}, u32[]{:S(2)}) collective-permute-start(f32[3,10,1]{2,1,0:T(8,128)S(1)} %get-tuple-element.24), channel_id=1, source_target_pairs={{0,1},{1,2},{2,3},{4,5},{5,6},{6,7},{8,9},{9,10},{10,11},{12,13},{... | collective-permute-start | bytes 368 | tf_op jit(solution)/shard_map/ppermute | solution.py:18
  149.3 3.9 %collective-permute-start.10 = (f32[3,10,1]{2,1,0:T(8,128)S(1)}, f32[3,10,1]{2,1,0:T(8,128)S(1)}, u32[]{:S(2)}, u32[]{:S(2)}) collective-permute-start(f32[3,10,1]{2,1,0:T(8,128)S(1)} %get-tuple-element.23), channel_id=1, source_target_pairs={{1,0},{2,1},{3,2},{5,4},{6,5},{7,6},{9,8},{10,9},{11,10},{13,12},{... | collective-permute-start | bytes 368 | tf_op jit(solution)/shard_map/ppermute | solution.py:19
where the time goes:
time: 199 us; the launch traced here: 198 us
  blocking collectives  141 us (71%)
  starting transfers between devices  29.2 us (15%)
  waiting for transfers between devices  10 us (5%)
  between operations  6.67 us (3%)
  local copies, waits for them, and re-layouts  5.22 us (3%)
  other arithmetic  3.45 us (2%)
  matrix products  2.83 us (1%)
    psum x1, blocking collectives, on_device(): curve_sum = lax.psum(jnp.sum(direction * applied), ('row', 'col'))  43 us
    psum x1, blocking collectives, on_device(): lax.psum((jnp.sum(direction * applied), jnp.dot(basis_rows, applied.resha...  42.6 us
    psum x1, blocking collectives, on_device(): lax.psum((jnp.dot(basis_rows, residual.reshape(-1), precision=high), jnp....  41.9 us
    ppermute x6, starting transfers between devices, padded_2(): before = lax.ppermute(last, axis, up)  21.5 us
    unnamed x2, blocking collectives  13.4 us
    ppermute x6, starting transfers between devices, padded_2(): after = lax.ppermute(leading, axis, down)  7.73 us
    ppermute x6, waiting for transfers between devices, padded_2(): after = lax.ppermute(leading, axis, down)  6.67 us
    unnamed x19, local copies, waits for them, and re-layouts  4.22 us
  transfers between devices with their start and end apart: 12, of which 5 were waited for; matrix products, arithmetic and copies ran while one was open for 2% of the time, Pallas kernels for 0%

commit v1 on v0

v1 whole, which is shorter than its diff:
```python
import functools
import math

import jax
import jax.numpy as jnp
from jax import lax
from jax.experimental import pallas as pl
from jax.experimental.pallas import tpu as pltpu
from jax.sharding import PartitionSpec as P

MESH = pl.DeviceIdType.MESH
HIGH = lax.Precision.HIGHEST
F32 = jnp.float32
OPPOSITE = (1, 0, 3, 2)


def total_row(parts, sums, lanes):
    rows = list(parts)
    held = sum(p.shape[0] for p in rows)
    if sums:
        rows += [s for s in sums]
        held += len(sums)
    rows.append(jnp.zeros((lanes - held, rows[0].shape[1]), F32))
    stacked = jnp.concatenate(rows, axis=0)
    ones = jnp.ones((8, stacked.shape[1]), F32)
    return lax.dot_general(
        ones, stacked, (((1,), (1,)), ((), ())), precision=HIGH, preferred_element_type=F32
    )[0:1]


def kernel(
    nrow,
    ncol,
    scale,
    r_ref,
    visc_ref,
    mask_ref,
    basis_ref,
    gram_ref,
    sol_ref,
    res_ref,
    basis_t,
    row_recv,
    col_send,
    col_recv,
    edge_send,
    edge_recv,
    gram_full,
    sum_send,
    sum_recv,
    load_sem,
    row_ssem,
    row_rsem,
    col_ssem,
    col_rsem,
    edge_ssem,
    edge_rsem,
    gram_ssem,
    gram_rsem,
    sum_ssem,
    sum_rsem,
):
    comps, rows, lanes = r_ref.shape
    basis = basis_ref.shape[0]
    cells = comps * rows
    n = nrow * ncol
    my_row, my_col = lax.axis_index("row"), lax.axis_index("col")
    me = my_row * ncol + my_col
    has = (my_row < nrow - 1, my_row > 0, my_col < ncol - 1, my_col > 0)
    where_to = (
        (my_row + 1, my_col),
        (my_row - 1, my_col),
        (my_row, my_col + 1),
        (my_row, my_col - 1),
    )

    loads = [
        pltpu.make_async_copy(
            basis_ref.at[:, c, r], basis_t.at[c, r], load_sem.at[c * rows + r]
        )
        for c in range(comps)
        for r in range(rows)
    ]
    for load in loads:
        load.start()

    barrier = pltpu.get_barrier_semaphore()

    def greet(i, carry):
        t = lax.rem(me + i, n)
        pl.semaphore_signal(
            barrier, inc=1, device_id=(t // ncol, lax.rem(t, ncol)), device_id_type=MESH
        )
        return carry

    lax.fori_loop(1, n, greet, 0)

    for d in range(4):

        @pl.when(jnp.logical_not(has[d]))
        def _(d=d):
            for stage in range(3):
                edge_recv[stage, d] = jnp.zeros(edge_recv.shape[2:], F32)
            if d < 2:
                row_recv[d] = jnp.zeros(row_recv.shape[1:], F32)
            else:
                col_recv[d - 2] = jnp.zeros(col_recv.shape[1:], F32)

    lane_of = lax.broadcasted_iota(jnp.int32, (rows, lanes), 1)
    row_of = lax.broadcasted_iota(jnp.int32, (rows, lanes), 0)
    diag_mask = [lane_of == row_of + c * rows for c in range(comps)]
    wide_lane = lax.broadcasted_iota(jnp.int32, (basis, lanes), 1)

    def col_to_row(cols):
        out = None
        for c, col in enumerate(cols):
            term = jnp.sum(
                jnp.where(diag_mask[c], jnp.broadcast_to(col, (rows, lanes)), 0.0),
                axis=0,
                keepdims=True,
            )
            out = term if out is None else out + term
        return out

    def row_to_cols(row):
        wide = jnp.broadcast_to(row, (rows, lanes))
        return [
            jnp.sum(jnp.where(diag_mask[c], wide, 0.0), axis=1, keepdims=True)
            for c in range(comps)
        ]

    def shifted(x, north, south, east, west):
        return (
            jnp.where(row_of == rows - 1, north, pltpu.roll(x, rows - 1, axis=0)),
            jnp.where(row_of == 0, south, pltpu.roll(x, 1, axis=0)),
            jnp.where(lane_of == lanes - 1, east, pltpu.roll(x, lanes - 1, axis=1)),
            jnp.where(lane_of == 0, west, pltpu.roll(x, 1, axis=1)),
        )

    def edge_copy(stage, d):
        return pltpu.make_async_remote_copy(
            src_ref=edge_send.at[stage, d],
            dst_ref=edge_recv.at[stage, OPPOSITE[d]],
            send_sem=edge_ssem.at[stage, d],
            recv_sem=edge_rsem.at[stage, OPPOSITE[d]],
            device_id=where_to[d],
            device_id_type=MESH,
        )

    def edge_arrival(stage, d):
        return pltpu.make_async_remote_copy(
            src_ref=edge_send.at[stage, d],
            dst_ref=edge_recv.at[stage, d],
            send_sem=edge_ssem.at[stage, d],
            recv_sem=edge_rsem.at[stage, d],
            device_id=where_to[d],
            device_id_type=MESH,
        )

    def send_edges(stage):
        for d in range(4):
            pl.when(has[d])(edge_copy(stage, d).start)

    def wait_edges(stage):
        for d in range(4):
            pl.when(has[d])(edge_arrival(stage, d).wait_recv)

    def put_edge(stage, d, x, slot):
        if d < 2:
            at = rows - 1 if d == 0 else 0
            for c, part in enumerate(x):
                edge_send[stage, d, slot + c : slot + c + 1] = part[at : at + 1]
        else:
            at = lanes - 1 if d == 2 else 0
            edge_send[stage, d, slot : slot + 1] = col_to_row(
                [part[:, at : at + 1] for part in x]
            )

    def send_sums(phase, row):
        sum_send[phase] = row
        sum_recv[phase, me] = row

        def send(i, carry):
            t = lax.rem(me + i, n)
            pltpu.make_async_remote_copy(
                src_ref=sum_send.at[phase],
                dst_ref=sum_recv.at[phase, me],
                send_sem=sum_ssem.at[phase],
                recv_sem=sum_rsem.at[phase],
                device_id=(t // ncol, lax.rem(t, ncol)),
                device_id_type=MESH,
            ).start()
            return carry

        lax.fori_loop(1, n, send, 0)

    def wait_sums(phase):
        others = sum_recv.at[phase, pl.ds(0, n - 1)]
        pltpu.make_async_copy(others, others, sum_rsem.at[phase]).wait()
        return jnp.sum(sum_recv[phase], axis=0)

    def project(x):
        acc = None
        for c in range(comps):
            for r in range(rows):
                term = basis_t[c, r] * x[c][r : r + 1]
                acc = term if acc is None else acc + term
        return acc

    def lift(block, coeffs):
        return jnp.sum(block * coeffs, axis=0, keepdims=True)

    def lift_all(coeffs):
        return [
            jnp.concatenate([lift(basis_t[c, r], coeffs) for r in range(rows)], axis=0)
            for c in range(comps)
        ]

    def inner(xs, ys):
        out = None
        for x, y in zip(xs, ys):
            term = jnp.sum(x * y, axis=0, keepdims=True)
            out = term if out is None else out + term
        return out

    gram_full[my_col] = gram_ref[...]
    right = [r_ref[c] for c in range(comps)]
    free = [mask_ref[c].astype(F32) for c in range(comps)]
    visc = visc_ref[...]
    for d in range(4):
        slots = (0, comps, 2 * comps) if d < 2 else (0, 1, 2)
        put_edge(0, d, [visc], slots[2])
        put_edge(0, d, right, slots[0])
        put_edge(0, d, free, slots[1])

    for load in loads:
        load.wait()
    first = total_row([project(right)], [], lanes)

    pl.semaphore_wait(barrier, n - 1)
    send_sums(0, first)
    send_edges(0)

    def row_copy(d, dst):
        return pltpu.make_async_remote_copy(
            src_ref=basis_t.at[:, rows - 1 if d == 0 else 0],
            dst_ref=row_recv.at[dst],
            send_sem=row_ssem.at[d],
            recv_sem=row_rsem.at[dst],
            device_id=where_to[d],
            device_id_type=MESH,
        )

    def col_copy(d, dst):
        return pltpu.make_async_remote_copy(
            src_ref=col_send.at[d - 2],
            dst_ref=col_recv.at[dst - 2],
            send_sem=col_ssem.at[d - 2],
            recv_sem=col_rsem.at[dst - 2],
            device_id=where_to[d],
            device_id_type=MESH,
        )

    for d in range(2):
        pl.when(has[d])(row_copy(d, OPPOSITE[d]).start)

    def gram_copy(i):
        return pltpu.make_async_remote_copy(
            src_ref=gram_ref,
            dst_ref=gram_full.at[my_col],
            send_sem=gram_ssem,
            recv_sem=gram_rsem,
            device_id=(my_row, lax.rem(my_col + i, ncol)),
            device_id_type=MESH,
        )

    for i in range(1, ncol):
        gram_copy(i).start()

    for d in (2, 3):
        at = lanes - 1 if d == 2 else 0
        gathered = jnp.zeros((basis, lanes), F32)
        for c in range(comps):
            for r in range(rows):
                spot = c * rows + r
                turned = pltpu.roll(basis_t[c, r], (spot - at) % lanes, axis=1)
                gathered = jnp.where(wide_lane == spot, turned, gathered)
        col_send[d - 2] = gathered
        pl.when(has[d])(col_copy(d, OPPOSITE[d]).start)

    wait_edges(0)
    visc_halo = [edge_recv[0, d, 2 * comps : 2 * comps + 1] for d in range(2)]
    for d in (2, 3):
        visc_halo.append(row_to_cols(edge_recv[0, d, 2:3])[0])
    faces = [0.5 * (visc + v) for v in shifted(visc, *visc_halo)]
    diagonal = 1.0 + faces[0] + faces[1] + faces[2] + faces[3]
    inverse = 1.0 / diagonal
    scaled = [u * inverse for u in free]
    jacobi = [s + (1.0 - u) for s, u in zip(scaled, free)]
    for d in range(4):
        put_edge(1, d, scaled, 0)
    send_edges(1)

    def operate(x, halo):
        out = []
        for c in range(comps):
            masked = free[c] * x[c]
            around = shifted(masked, *[halo[d][c] for d in range(4)])
            stencil = diagonal * masked - (
                faces[0] * around[0]
                + faces[1] * around[1]
                + faces[2] * around[2]
                + faces[3] * around[3]
            )
            out.append(free[c] * stencil + (1.0 - free[c]) * x[c])
        return out

    def halos(coeffs, step):
        out = []
        for d in range(4):
            if d < 2:
                rows_out = []
                for c in range(comps):
                    res = edge_recv[0, d, c : c + 1]
                    if step is not None:
                        res = res - step * edge_recv[2, d, c : c + 1]
                    rows_out.append(
                        edge_recv[1, d, c : c + 1] * res
                        + edge_recv[0, d, comps + c : comps + c + 1]
                        * lift(row_recv[d, c], coeffs)
                    )
                out.append(rows_out)
            else:
                res = edge_recv[0, d, 0:1]
                if step is not None:
                    res = res - step * edge_recv[2, d, 0:1]
                row = edge_recv[1, d, 0:1] * res + edge_recv[0, d, 1:2] * lift(
                    col_recv[d - 2], coeffs
                )
                out.append(row_to_cols(row))
        return out

    for d in range(4):
        if d < 2:
            pl.when(has[d])(row_copy(d, d).wait_recv)
        else:
            pl.when(has[d])(col_copy(d, d).wait_recv)
    others = gram_full.at[pl.ds(0, ncol - 1)]
    pltpu.make_async_copy(others, others, gram_rsem).wait()
    gram = gram_full[...].reshape(basis, basis)
    wait_edges(1)

    def solve(dot):
        return jnp.sum(gram * dot[:, :basis], axis=1, keepdims=True) * scale

    dot = wait_sums(0)
    coeffs = solve(dot)
    direction = [j * r + b for j, r, b in zip(jacobi, right, lift_all(coeffs))]
    image = operate(direction, halos(coeffs, None))
    for d in range(4):
        put_edge(2, d, image, 0)
    send_edges(2)
    second = total_row(
        [project(image)], [inner(right, direction), inner(direction, image)], lanes
    )
    send_sums(1, second)
    wait_edges(2)
    sums = wait_sums(1)
    energy = sums[:, basis : basis + 1]
    curve = sums[:, basis + 1 : basis + 2]
    step = energy / curve
    residual = [r - step * w for r, w in zip(right, image)]
    coeffs = solve(dot - step * sums)
    smoothed = [j * r + b for j, r, b in zip(jacobi, residual, lift_all(coeffs))]
    smoothed_image = operate(smoothed, halos(coeffs, step))
    third = total_row(
        [],
        [
            inner(residual, smoothed),
            inner(smoothed, image),
            inner(smoothed, smoothed_image),
        ],
        lanes,
    )
    send_sums(2, third)
    sums = wait_sums(2)
    energy_new = sums[:, 0:1]
    ratio = energy_new / energy
    curve_new = sums[:, 2:3] + ratio * (2.0 * sums[:, 1:2] + ratio * curve)
    step_new = energy_new / curve_new
    for c in range(comps):
        sol_ref[c] = step * direction[c] + step_new * (smoothed[c] + ratio * direction[c])
        res_ref[c] = residual[c] - step_new * (smoothed_image[c] + ratio * image[c])

    for phase in range(3):
        sent = sum_recv.at[phase, pl.ds(0, n - 1)]
        pltpu.make_async_copy(sent, sent, sum_ssem.at[phase]).wait()
    others = gram_full.at[pl.ds(0, ncol - 1)]
    pltpu.make_async_copy(others, others, gram_ssem).wait()
    for d in range(4):
        for stage in range(3):
            pl.when(has[d])(edge_copy(stage, d).wait_send)
        if d < 2:
            pl.when(has[d])(row_copy(d, d).wait_send)
        else:
            pl.when(has[d])(col_copy(d, d).wait_send)


def on_device(nrow, ncol, right_side, viscosity, free_mask, coarse_basis, gram_inverse):
    comps, rows, lanes = right_side.shape
    basis = coarse_basis.shape[0]
    n = nrow * ncol
    unknowns = comps * rows * lanes * n * basis
    scale = 1.0 / (32.0 * math.sqrt(float(unknowns)))
    vmem = pl.BlockSpec(memory_space=pltpu.VMEM)
    dma = pltpu.SemaphoreType.DMA
    return pl.pallas_call(
        functools.partial(kernel, nrow, ncol, scale),
        out_shape=[jax.ShapeDtypeStruct(right_side.shape, F32)] * 2,
        in_specs=[vmem, vmem, vmem, pl.BlockSpec(memory_space=pl.ANY), vmem],
        out_specs=[vmem, vmem],
        scratch_shapes=[
            pltpu.VMEM((comps, rows, basis, lanes), F32),
            pltpu.VMEM((2, comps, basis, lanes), F32),
            pltpu.VMEM((2, basis, lanes), F32),
            pltpu.VMEM((2, basis, lanes), F32),
            pltpu.VMEM((3, 4, 8, lanes), F32),
            pltpu.VMEM((3, 4, 8, lanes), F32),
            pltpu.VMEM((ncol,) + gram_inverse.shape, F32),
            pltpu.VMEM((3, 1, lanes), F32),
            pltpu.VMEM((3, n, 1, lanes), F32),
            dma((comps * rows,)),
            dma((2,)),
            dma((2,)),
            dma((2,)),
            dma((2,)),
            dma((3, 4)),
            dma((3, 4)),
            dma,
            dma,
            dma((3,)),
            dma((3,)),
        ],
        compiler_params=pltpu.CompilerParams(
            collective_id=0, has_side_effects=True, vmem_limit_bytes=48 * 1024 * 1024
        ),
    )(right_side, viscosity, free_mask, coarse_basis, gram_inverse)


def solution(mesh):
    in_specs = (
        P(None, "row", "col"),
        P("row", "col"),
        P(None, "row", "col"),
        P(None, None, "row", "col"),
        P("col", None),
    )
    out_specs = (P(None, "row", "col"), P(None, "row", "col"))
    return jax.shard_map(
        functools.partial(on_device, mesh.shape["row"], mesh.shape["col"]),
        mesh=mesh,
        in_specs=in_specs,
        out_specs=out_specs,
        check_vma=False,
    )
```

time: 199 us -> 32.7 us (0.16)
  blocking collectives: 141 us -> 0 us
  starting transfers between devices: 29.2 us -> 0 us
  Pallas kernels: 0 us -> 26.6 us
  waiting for transfers between devices: 10 us -> 0 us
  between operations: 6.67 us -> 0.65 us
  other arithmetic: 3.45 us -> 0 us
  matrix products: 2.83 us -> 0 us
    psum x3 -> x0, blocking collectives: 127 us -> none  [the longest x1 43 us: on_device(): curve_sum = lax.psum(jnp.sum(direction * applied), ('row', 'col'))]
    ppermute x12 -> x0, starting transfers between devices: 29.2 us -> none  [the longest x6 21.5 us: padded_2(): before = lax.ppermute(last, axis, up)]
    pallas_call x0 -> x1, Pallas kernels: none -> 26.6 us  [on_device(): pl.pallas_call(functools.partial(kernel, nrow, ncol, scale), out_shape=[j...]
    unnamed x2 -> x0, blocking collectives: 13.4 us -> none
    ppermute x12 -> x0, waiting for transfers between devices: 10 us -> none  [the longest x6 6.67 us: padded_2(): after = lax.ppermute(leading, axis, down)]
    dot_general x6 -> x0, matrix products: 2.83 us -> none  [the longest x2 1.13 us: precondition(): jnp.dot(coeffs, basis_rows, precision=high).reshape(residual.shape)]
    unnamed x19 -> x12, local copies, waits for them, and re-layouts: 4.22 us -> 5.12 us
  transfers between devices with their start and end apart: 12 -> 0, of which waited for: 5 -> 0; matrix products, arithmetic and copies ran while one was open for 2% -> 0% of each run, Pallas kernels for 0% -> 0%
where the time goes in v1:
time: 32.7 us; the launch traced here: 32.3 us
  Pallas kernels  26.6 us (81%)
  local copies, waits for them, and re-layouts  5.12 us (16%)
  between operations  0.65 us (2%)
    pallas_call x1, Pallas kernels, on_device(): pl.pallas_call(functools.partial(kernel, nrow, ncol, scale), out_shape=[j...  26.6 us
    unnamed x12, local copies, waits for them, and re-layouts  5.12 us

profile of v1, /device:TPU:0, one launch (start us, length us, event | category | flops | bytes accessed | tf_op | source)
XLA Modules:
  0.0 32.3 jit_solution(8183664396629269946)
XLA Ops:
  0.6 0.0 copy-start
  0.6 1.1 %copy-done = f32[64,3,8,128]{3,2,1,0:T(8,128)S(1)} copy-done((f32[64,3,8,128]{3,2,1,0:T(8,128)S(1)}, f32[64,3,8,128]{3,2,1,0:T(8,128)}, u32[]{:S(2)}) %copy-start) | copy-done | bytes 786456
  1.8 0.0 copy-start.1
  1.8 0.7 %copy-done.1 = f32[3,8,128]{2,1,0:T(8,128)S(1)} copy-done((f32[3,8,128]{2,1,0:T(8,128)S(1)}, f32[3,8,128]{2,1,0:T(8,128)}, u32[]{:S(2)}) %copy-start.1) | copy-done | bytes 12312
  2.5 0.0 copy-start.2
  2.5 0.7 %copy-done.2 = s32[3,8,128]{2,1,0:T(8,128)S(1)} copy-done((s32[3,8,128]{2,1,0:T(8,128)S(1)}, s32[3,8,128]{2,1,0:T(8,128)}, u32[]{:S(2)}) %copy-start.2) | copy-done | bytes 12312
  3.2 0.0 copy-start.3
  3.2 0.7 %copy-done.3 = f32[16,64]{1,0:T(8,128)S(1)} copy-done((f32[16,64]{1,0:T(8,128)S(1)}, f32[16,64]{1,0:T(8,128)}, u32[]{:S(2)}) %copy-start.3) | copy-done | bytes 4120
  3.9 0.0 copy-start.4
  3.9 0.7 %copy-done.4 = f32[8,128]{1,0:T(8,128)S(1)} copy-done((f32[8,128]{1,0:T(8,128)S(1)}, f32[8,128]{1,0:T(8,128)}, u32[]{:S(2)}) %copy-start.4) | copy-done | bytes 4120
  4.6 26.6 %shard_map.68 = (f32[3,8,128]{2,1,0:T(8,128)S(1)}, f32[3,8,128]{2,1,0:T(8,128)S(1)}) custom-call(f32[3,8,128]{2,1,0:T(8,128)S(1)} %copy-done.1, f32[8,128]{1,0:T(8,128)S(1)} %copy-done.4, s32[3,8,128]{2,1,0:T(8,128)S(1)} %copy-done.2, f32[64,3,8,128]{3,2,1,0:T(8,128)S(1)} %copy-done, f32[16,64]{1,0:T(8,128)S(1)} %copy-done.3), custom_call_target="tpu_custom_call" | custom-call | tf_op jit(solution)/shard_map/pallas_call | solution.py:417
  31.1 0.6 %copy.9 = f32[3,8,128]{2,1,0:T(8,128)} copy(f32[3,8,128]{2,1,0:T(8,128)S(1)} %get-tuple-element.4) | data formatting | bytes 24576
  31.7 0.6 %copy.10 = f32[3,8,128]{2,1,0:T(8,128)} copy(f32[3,8,128]{2,1,0:T(8,128)S(1)} %get-tuple-element.5) | data formatting | bytes 24576
Async XLA Ops:
  0.6 1.1 %copy-start = (f32[64,3,8,128]{3,2,1,0:T(8,128)S(1)}, f32[64,3,8,128]{3,2,1,0:T(8,128)}, u32[]{:S(2)}) copy-start(f32[64,3,8,128]{3,2,1,0:T(8,128)} %basis_ref.1) | copy-start | bytes 2359300
  1.8 0.7 %copy-start.1 = (f32[3,8,128]{2,1,0:T(8,128)S(1)}, f32[3,8,128]{2,1,0:T(8,128)}, u32[]{:S(2)}) copy-start(f32[3,8,128]{2,1,0:T(8,128)} %r_ref.1) | copy-start | bytes 36868
  2.5 0.7 %copy-start.2 = (s32[3,8,128]{2,1,0:T(8,128)S(1)}, s32[3,8,128]{2,1,0:T(8,128)}, u32[]{:S(2)}) copy-start(s32[3,8,128]{2,1,0:T(8,128)} %mask_ref.1) | copy-start | bytes 36868
  3.2 0.7 %copy-start.3 = (f32[16,64]{1,0:T(8,128)S(1)}, f32[16,64]{1,0:T(8,128)}, u32[]{:S(2)}) copy-start(f32[16,64]{1,0:T(8,128)} %gram_ref.1) | copy-start | bytes 12292
  3.9 0.7 %copy-start.4 = (f32[8,128]{1,0:T(8,128)S(1)}, f32[8,128]{1,0:T(8,128)}, u32[]{:S(2)}) copy-start(f32[8,128]{1,0:T(8,128)} %visc_ref.1) | copy-start | bytes 12292

commit v2 on v1

--- a/solution.py
+++ b/solution.py
@@ -32,13 +32,17 @@
     nrow,
     ncol,
     scale,
+    r_hbm,
+    visc_hbm,
+    mask_hbm,
+    basis_ref,
+    gram_hbm,
+    sol_ref,
+    res_ref,
     r_ref,
     visc_ref,
     mask_ref,
-    basis_ref,
     gram_ref,
-    sol_ref,
-    res_ref,
     basis_t,
     row_recv,
     col_send,
@@ -49,6 +53,7 @@
     sum_send,
     sum_recv,
     load_sem,
+    small_sem,
     row_ssem,
     row_rsem,
     col_ssem,
@@ -81,7 +86,18 @@
         for c in range(comps)
         for r in range(rows)
     ]
-    for load in loads:
+    small = [
+        pltpu.make_async_copy(src, dst, small_sem.at[i])
+        for i, (src, dst) in enumerate(
+            (
+                (r_hbm, r_ref),
+                (visc_hbm, visc_ref),
+                (mask_hbm, mask_ref),
+                (gram_hbm, gram_ref),
+            )
+        )
+    ]
+    for load in small + loads:
         load.start()
 
     barrier = pltpu.get_barrier_semaphore()
@@ -223,6 +239,8 @@
             out = term if out is None else out + term
         return out
 
+    for load in small:
+        load.wait()
     gram_full[my_col] = gram_ref[...]
     right = [r_ref[c] for c in range(comps)]
     free = [mask_ref[c].astype(F32) for c in range(comps)]
@@ -417,9 +435,13 @@
     return pl.pallas_call(
         functools.partial(kernel, nrow, ncol, scale),
         out_shape=[jax.ShapeDtypeStruct(right_side.shape, F32)] * 2,
-        in_specs=[vmem, vmem, vmem, pl.BlockSpec(memory_space=pl.ANY), vmem],
+        in_specs=[pl.BlockSpec(memory_space=pltpu.HBM)] * 5,
         out_specs=[vmem, vmem],
         scratch_shapes=[
+            pltpu.VMEM(right_side.shape, F32),
+            pltpu.VMEM(viscosity.shape, F32),
+            pltpu.VMEM(free_mask.shape, free_mask.dtype),
+            pltpu.VMEM(gram_inverse.shape, F32),
             pltpu.VMEM((comps, rows, basis, lanes), F32),
             pltpu.VMEM((2, comps, basis, lanes), F32),
             pltpu.VMEM((2, basis, lanes), F32),
@@ -430,6 +452,7 @@
             pltpu.VMEM((3, 1, lanes), F32),
             pltpu.VMEM((3, n, 1, lanes), F32),
             dma((comps * rows,)),
+            dma((4,)),
             dma((2,)),
             dma((2,)),
             dma((2,)),
@@ -442,7 +465,7 @@
             dma((3,)),
         ],
         compiler_params=pltpu.CompilerParams(
-            collective_id=0, has_side_effects=True, vmem_limit_bytes=48 * 1024 * 1024
+            collective_id=0, has_side_effects=True, vmem_limit_bytes=67_043_328
         ),
     )(right_side, viscosity, free_mask, coarse_basis, gram_inverse)
 

time: 32.7 us -> 29.5 us (0.902)
  local copies, waits for them, and re-layouts: 5.12 us -> 1.92 us
    unnamed x12 -> x4, local copies, waits for them, and re-layouts: 5.12 us -> 1.92 us
where the time goes in v2:
time: 29.5 us; the launch traced here: 29.3 us
  Pallas kernels  26.7 us (91%)
  local copies, waits for them, and re-layouts  1.92 us (7%)
  between operations  0.65 us (2%)
    pallas_call x1, Pallas kernels, on_device(): pl.pallas_call(functools.partial(kernel, nrow, ncol, scale), out_shape=[j...  26.7 us
    unnamed x4, local copies, waits for them, and re-layouts  1.92 us

profile of v2, /device:TPU:0, one launch (start us, length us, event | category | flops | bytes accessed | tf_op | source)
XLA Modules:
  0.0 29.3 jit_solution(490445609294477772)
XLA Ops:
  0.6 26.7 %shard_map.68 = (f32[3,8,128]{2,1,0:T(8,128)}, f32[3,8,128]{2,1,0:T(8,128)}) custom-call(f32[3,8,128]{2,1,0:T(8,128)} %r_hbm.1, f32[8,128]{1,0:T(8,128)} %visc_hbm.1, s32[3,8,128]{2,1,0:T(8,128)} %mask_hbm.1, f32[64,3,8,128]{3,2,1,0:T(8,128)} %basis_ref.1, f32[16,64]{1,0:T(8,128)} %gram_hbm.1), custom_call_target="tpu_custom_call" | custom-call | tf_op jit(solution)/shard_map/pallas_call | solution.py:435
  27.3 0.0 copy-start
  27.3 1.3 %copy.9 = f32[3,8,128]{2,1,0:T(8,128)} copy(f32[3,8,128]{2,1,0:T(8,128)} %get-tuple-element.4) | data formatting | bytes 24576
  28.6 0.0 copy-done
  28.7 0.6 %copy.10 = f32[3,8,128]{2,1,0:T(8,128)} copy(f32[3,8,128]{2,1,0:T(8,128)S(1)} %copy-done) | data formatting | bytes 24576
Async XLA Ops:
  27.3 1.3 %copy-start = (f32[3,8,128]{2,1,0:T(8,128)S(1)}, f32[3,8,128]{2,1,0:T(8,128)}, u32[]{:S(2)}) copy-start(f32[3,8,128]{2,1,0:T(8,128)} %get-tuple-element.5) | copy-start | bytes 36868
